TPU v7x, 32 devices: a whole 2x2x4 slice. The times are simulated.
32 devices in a mesh: span: 4 (over y, x), heads: 8 (over z, core).
Axes of the slice: x: 2, y: 2, z: 4, core: 2. Of those that a mesh axis runs over, the one named last changes fastest.
Arguments:
- latents: bfloat16 [4, 6144, 512], P(None, ('span', 'heads')), may hold values from -6 to 6
- rotary_rows: bfloat16 [4, 6144, 64], P(None, ('span', 'heads')), may hold values from -6 to 6
- latent_gain: float32 [512], replicated, may hold values from 0.25 to 1.75
- key_up: bfloat16 [512, 16, 128], P(None, 'heads'), may hold values from -0.25 to 0.25
- value_up: bfloat16 [512, 16, 128], P(None, 'heads'), may hold values from -0.25 to 0.25
Outputs:
- stored_keys: bfloat16 [4, 6144, 16, 192], P('span', None, 'heads')
- stored_values: bfloat16 [4, 6144, 16, 128], P('span', None, 'heads')
All inputs are finite; a program needn't handle non-finite values.
Results may differ from a plain program's by a relative error of at most 0.001.
Values may be sent and summed in bfloat16 or wider, within the bound.
A program may use at most 128 MiB of HBM per device.

v0:
```python
import jax
import jax.numpy as jnp
from jax import lax
from jax.sharding import PartitionSpec as P


def expand_rows(rows, rotary, key_up, value_up):
    wide_keys = jnp.einsum(
        "btr,rhk->bthk", rows, key_up, preferred_element_type=jnp.float32
    ).astype(jnp.bfloat16)
    shared = jnp.broadcast_to(rotary[:, :, None], wide_keys.shape[:3] + rotary.shape[2:])
    wide_values = jnp.einsum(
        "btr,rhk->bthk", rows, value_up, preferred_element_type=jnp.float32
    ).astype(jnp.bfloat16)
    return (jnp.concatenate([wide_keys, shared], axis=-1), wide_values)


def root_norm(vectors, row_gain):
    return (
        vectors * lax.rsqrt(jnp.mean(vectors * vectors, axis=-1, keepdims=True) + 1e-06) * row_gain
    )


def per_device(latents, rotary_rows, latent_gain, key_up, value_up):
    rows_ready = root_norm(latents.astype(jnp.float32), latent_gain).astype(jnp.bfloat16)
    rows_moved, rotary_moved = (
        lax.all_to_all(rows_ready, "span", split_axis=0, concat_axis=1, tiled=True),
        lax.all_to_all(rotary_rows, "span", split_axis=0, concat_axis=1, tiled=True),
    )
    rows_cut = rows_moved.reshape(
        rows_moved.shape[0], lax.axis_size("span"), -1, rows_moved.shape[2]
    )
    rotary_cut = rotary_moved.reshape(
        rotary_moved.shape[0], lax.axis_size("span"), -1, rotary_moved.shape[2]
    )
    rows_joined, rotary_joined = (
        lax.all_gather(rows_cut, "heads", axis=2, tiled=True),
        lax.all_gather(rotary_cut, "heads", axis=2, tiled=True),
    )
    rows_whole = rows_joined.reshape(rows_joined.shape[0], -1, rows_joined.shape[3])
    rotary_whole = rotary_joined.reshape(rotary_joined.shape[0], -1, rotary_joined.shape[3])
    stored_keys, stored_values = expand_rows(rows_whole, rotary_whole, key_up, value_up)
    return (stored_keys, stored_values)


def solution(mesh):
    in_specs = (
        P(None, ("span", "heads"), None),
        P(None, ("span", "heads"), None),
        P(),
        P(None, "heads", None),
        P(None, "heads", None),
    )
    out_specs = (P("span", None, "heads", None), P("span", None, "heads", None))
    return jax.shard_map(
        per_device, mesh=mesh, in_specs=in_specs, out_specs=out_specs, check_vma=False
    )
```

profile of v0, /device:TPU:0, one launch (start us, length us, event | category | flops | bytes accessed | tf_op | source)
XLA Modules:
  0.0 148.6 jit_solution(12033314378571793330)
XLA Ops:
  7.2 0.0 copy-start
  7.2 0.0 copy-start.2
  7.2 0.0 all-gather.4.cloned.1.call-start
  7.2 1.4 fusion.1
  8.7 1.4 fusion.3
  10.1 16.5 %all_to_all.8 = bf16[4,192,512]{2,1,0:T(8,128)(2,1)} all-to-all(bf16[4,192,512]{2,1,0:T(8,128)(2,1)S(1)} %fusion.3), channel_id=1, replica_groups=mesh['span'=4,'heads'=8] {'span'}, dimensions={0} | all-to-all | bytes 1572864 | tf_op jit(solution)/shard_map/all_to_all | solution.py:27
  26.5 0.0 all-gather.4.cloned.1.call-update
  26.6 3.3 %all-to-all-start.1 = ((bf16[4,192,64]{1,2,0:T(8,128)(2,1)}), bf16[4,192,64]{1,2,0:T(8,128)(2,1)S(1)}, u32[]{:S(2)}, u32[]{:S(2)}) async-start(bf16[4,192,64]{1,2,0:T(8,128)(2,1)} %param.6), calls=%async_computation.1 | async-start | bytes 262144 | tf_op jit(solution)/shard_map/all_to_all | solution.py:28
  29.9 0.0 copy-done.2
  29.9 0.2 copy.19
  30.1 4.8 %all-to-all-done.1 = bf16[4,192,64]{1,2,0:T(8,128)(2,1)S(1)} async-done(((bf16[4,192,64]{1,2,0:T(8,128)(2,1)}), bf16[4,192,64]{1,2,0:T(8,128)(2,1)S(1)}, u32[]{:S(2)}, u32[]{:S(2)}) %all-to-all-start.1) | async-done | bytes 98336 | tf_op jit(solution)/shard_map/all_to_all | solution.py:28
  34.9 0.2 copy.20
  35.1 31.4 %all-gather.1 = bf16[4,1536,64]{2,0,1:T(4,128)(2,1)S(1)} all-gather(bf16[4,192,64]{2,0,1:T(4,128)(2,1)S(1)} %copy.20), channel_id=3, replica_groups=mesh['span'=4,'heads'=8] {'heads'}, dimensions={1}, use_global_device_ids=true | all-gather | bytes 884736 | tf_op jit(solution)/shard_map/all_gather | solution.py:38
  66.4 1.2 copy.21
  67.6 0.1 copy.24
  67.7 35.4 %all-gather.4.cloned.1.call-done = bf16[4,1536,512]{2,1,0:T(8,128)(2,1)} async-done(((bf16[4,192,512]{2,1,0:T(8,128)(2,1)}), bf16[4,1536,512]{2,1,0:T(8,128)(2,1)}) %all-gather.4.cloned.1.call-update) | async-done | bytes 6291472 | tf_op jit(solution)/shard_map/all_gather | solution.py:37
  103.1 4.6 %fusion.5 = f32[6144,256]{0,1:S(1)} fusion(bf16[6144,512]{1,0:T(8,128)(2,1)} %bitcast.17, bf16[512,256]{0,1:T(8,128)(2,1)S(1)} %bitcast.21), kind=kOutput, calls=%fused_computation.11 | convolution fusion | flops 1610612736 | bytes 12845056
  107.8 0.0 copy-start.1
  107.8 0.4 convert_bitcast_fusion
  108.2 2.3 %copy-done.1 = bf16[4,1536,512]{2,1,0:T(8,128)(2,1)S(1)} copy-done((bf16[4,1536,512]{2,1,0:T(8,128)(2,1)S(1)}, bf16[4,1536,512]{2,1,0:T(8,128)(2,1)}, u32[]{:S(2)}) %copy-start.1) | copy-done | bytes 6291480
  110.5 1.8 %fusion = bf16[1,6144,2,128]{3,1,2,0:T(8,128)(2,1)S(1)} fusion(bf16[6144,512,1]{1,0,2:T(8,128)(2,1)S(1)} %bitcast.18, bf16[512,2,128]{2,1,0:T(2,128)(2,1)S(1)} %copy-done), kind=kOutput, calls=%fused_computation.1 | convolution fusion | flops 1612185600 | bytes 9699328 | tf_op jit(solution)/shard_map/btr,rhk->bthk/dot_general | solution.py:12
  112.3 26.8 %copy.23 = bf16[1,6144,2,128]{3,2,1,0:T(2,128)(2,1)} copy(bf16[1,6144,2,128]{3,1,2,0:T(8,128)(2,1)S(1)} %fusion) | data formatting | bytes 6291456
  139.1 0.1 broadcast_in_dim.10
  139.3 2.5 %pad_maximum_fusion = bf16[1,6144,2,192]{1,3,2,0:T(8,128)(2,1)} fusion(bf16[1,6144,2,64]{1,3,2,0:T(8,128)(2,1)S(1)} %broadcast_in_dim.10, bf16[1,6144,2,128]{1,3,2,0:T(8,128)(2,1)S(1)} %convert_bitcast_fusion), kind=kLoop, calls=%fused_computation.2 | loop fusion | flops 9437184 | bytes 9437184 | tf_op jit(solution)/shard_map/concatenate | solution.py:15
  (2 shorter events, 0.0 us)
Async XLA Ops:
  7.2 101.0 %copy-start = (bf16[512,2,128]{2,1,0:T(2,128)(2,1)S(1)}, bf16[512,2,128]{2,1,0:T(2,128)(2,1)}, u32[]{:S(2)}) copy-start(bf16[512,2,128]{2,1,0:T(2,128)(2,1)} %param.9) | copy-start | bytes 786436
  7.2 22.7 %copy-start.2 = (bf16[512,2,128]{2,1,0:T(2,128)(2,1)S(1)}, bf16[512,2,128]{2,1,0:T(2,128)(2,1)}, u32[]{:S(2)}) copy-start(bf16[512,2,128]{2,1,0:T(2,128)(2,1)} %param.8) | copy-start | bytes 786436
  7.2 95.9 %all-gather.4.cloned.1.call-start = ((), (), s32[]{:S(2)}) async-start(), calls=%async_computation.2 | async-start | bytes 7077888 | tf_op jit(solution)/shard_map/all_gather | solution.py:37
  26.6 8.3 %all-to-all-start.1 = ((bf16[4,192,64]{1,2,0:T(8,128)(2,1)}), bf16[4,192,64]{1,2,0:T(8,128)(2,1)S(1)}, u32[]{:S(2)}, u32[]{:S(2)}) async-start(bf16[4,192,64]{1,2,0:T(8,128)(2,1)} %param.6), calls=%async_computation.1 | async-start | bytes 262144 | tf_op jit(solution)/shard_map/all_to_all | solution.py:28
  107.8 2.8 %copy-start.1 = (bf16[4,1536,512]{2,1,0:T(8,128)(2,1)S(1)}, bf16[4,1536,512]{2,1,0:T(8,128)(2,1)}, u32[]{:S(2)}) copy-start(bf16[4,1536,512]{2,1,0:T(8,128)(2,1)} %all-gather.4.cloned.1.call-done) | copy-start | bytes 18874372
Sparse Core Ops, SparseCore 0:
  26.7 76.4 all-gather.3
where the time goes:
time: 149 us
  blocking collectives  47.8 us (32%)
  waiting for transfers between devices  40.2 us (27%)
  local copies, waits for them, and re-layouts  30.9 us (21%)
  between operations  14.2 us (10%)
  matrix products  6.41 us (4%)
  other arithmetic  5.74 us (4%)
  starting transfers between devices  3.38 us (2%)
    all_gather x1, waiting for transfers between devices, per_device(): lax.all_gather(rows_cut, 'heads', axis=2, tiled=True)  35.4 us
    all_gather x1, blocking collectives, per_device(): lax.all_gather(rotary_cut, 'heads', axis=2, tiled=True)  31.4 us
    unnamed x9, local copies, waits for them, and re-layouts  29.4 us
    all_to_all x1, blocking collectives, per_device(): lax.all_to_all(rows_ready, 'span', split_axis=0, concat_axis=1, tiled=True)  16.5 us
    all_to_all x1, waiting for transfers between devices, per_device(): lax.all_to_all(rotary_rows, 'span', split_axis=0, concat_axis=1, tiled=True)  4.81 us
    unnamed x1, matrix products  4.61 us
    all_to_all x1, starting transfers between devices, per_device(): lax.all_to_all(rotary_rows, 'span', split_axis=0, concat_axis=1, tiled=True)  3.34 us
  transfers between devices with their start and end apart: 2, of which 2 were waited for; matrix products, arithmetic and copies ran while one was open for 1% of the time, Pallas kernels for 0%

commit v1 on v0

v1 whole, which is shorter than its diff:
```python
import functools

import jax
import jax.numpy as jnp
from jax import lax
from jax.experimental import pallas as pl
from jax.experimental.pallas import tpu as pltpu
from jax.sharding import PartitionSpec as P

MESH = pl.DeviceIdType.MESH
PIECES = 2


def gather_kernel(sizes, rows_ref, rotary_ref, rows_out, rotary_out, *sems):
    spans, chips, cores, pieces = sizes
    recv_sem, plane_sem, up_sem, down_sem, partner_sem, own_sem = sems
    block = rows_ref.shape[1]
    cut = block // pieces
    me_s = lax.axis_index("span")
    me_h = lax.axis_index("heads")
    z, c = me_h // cores, me_h % cores

    def span_of(i):
        if spans & (spans - 1):
            return (me_s + i) % spans
        total, bit = 0, 1
        while bit < spans:
            total = total + ((me_s // bit + i // bit) % 2) * bit
            bit *= 2
        return total

    def to(span, heads):
        return {"span": span, "heads": heads}

    def mine(span, piece):
        if piece < pieces:
            return rows_ref.at[span, pl.ds(piece * cut, cut)]
        return rotary_ref.at[span]

    def slot(span, chip, core, piece):
        if piece < pieces:
            return rows_out.at[span, chip * cores + core, pl.ds(piece * cut, cut)]
        return rotary_out.at[span, chip * cores + core]

    def arrived(span, chip, core, piece):
        return recv_sem.at[span, chip * cores + core, piece]

    def push(src, span, chip, piece, send_sem, device):
        return pltpu.make_async_remote_copy(
            src_ref=src,
            dst_ref=slot(span, chip, c, piece),
            send_sem=send_sem,
            recv_sem=arrived(span, chip, c, piece),
            device_id=device,
            device_id_type=MESH,
        )

    def wait_block(span, chip, core, piece):
        ref = slot(span, chip, core, piece)
        pltpu.make_async_remote_copy(
            src_ref=ref,
            dst_ref=ref,
            send_sem=arrived(span, chip, core, piece),
            recv_sem=arrived(span, chip, core, piece),
            device_id=to(me_s, me_h),
            device_id_type=MESH,
        ).wait_recv()

    up = lambda src, span, chip, p: push(
        src, span, chip, p, up_sem.at[span, chip, p], to(me_s, me_h + cores)
    )
    down = lambda src, span, chip, p: push(
        src, span, chip, p, down_sem.at[span, chip, p], to(me_s, me_h - cores)
    )
    across = lambda src, span, chip, p: push(
        src, span, chip, p, partner_sem.at[span, chip, p], to(me_s, z * cores + (c + 1) % cores)
    )
    has_up, has_down = z < chips - 1, z > 0

    barrier = pltpu.get_barrier_semaphore()

    def greet(device):
        pl.semaphore_signal(barrier, inc=1, device_id=device, device_id_type=MESH)

    for i in range(1, spans):
        greet(to(span_of(i), me_h))
    if cores > 1:
        greet(to(me_s, z * cores + (c + 1) % cores))
    pl.when(has_up)(lambda: greet(to(me_s, me_h + cores)))
    pl.when(has_down)(lambda: greet(to(me_s, me_h - cores)))
    peers = spans - 1 + (cores > 1) + jnp.where(has_up, 1, 0) + jnp.where(has_down, 1, 0)
    pl.semaphore_wait(barrier, peers)

    parts = range(pieces + 1)

    def plane(i, p):
        return pltpu.make_async_remote_copy(
            src_ref=mine(span_of(i), p),
            dst_ref=slot(me_s, z, c, p),
            send_sem=plane_sem.at[i, p],
            recv_sem=arrived(me_s, z, c, p),
            device_id=to(span_of(i), me_h),
            device_id_type=MESH,
        )

    def own(p):
        return pltpu.make_async_copy(mine(me_s, p), slot(me_s, z, c, p), own_sem.at[p])

    for p in parts:
        pl.when(has_up)(lambda: up(mine(me_s, p), me_s, z, p).start())
        pl.when(has_down)(lambda: down(mine(me_s, p), me_s, z, p).start())
    for p in parts:
        for i in range(1, spans):
            plane(i, p).start()
    for p in parts:
        own(p).start()
        if cores > 1:
            across(mine(me_s, p), me_s, z, p).start()

    def first(i, _):
        span = span_of(i)
        for p in parts:
            wait_block(span, z, c, p)
            src = slot(span, z, c, p)
            pl.when(has_up)(lambda: up(src, span, z, p).start())
            pl.when(has_down)(lambda: down(src, span, z, p).start())
            if cores > 1:
                across(src, span, z, p).start()
        return 0

    lax.fori_loop(1, spans, first, 0)

    def later(step, _):
        r, span = step // spans, span_of(step % spans)

        def pass_on(chip, further, send):
            for p in parts:
                wait_block(span, chip, c, p)
                src = slot(span, chip, c, p)
                pl.when(further)(lambda: send(src, span, chip, p).start())
                if cores > 1:
                    across(src, span, chip, p).start()

        pl.when(z - r >= 0)(lambda: pass_on(z - r, has_up, up))
        pl.when(z + r < chips)(lambda: pass_on(z + r, has_down, down))
        return 0

    lax.fori_loop(spans, spans * chips, later, 0)

    for p in parts:
        own(p).wait()
        for i in range(1, spans):
            plane(i, p).wait_send()

    def finish(step, _):
        span, chip = step % spans, step // spans
        for p in parts:
            src = slot(span, chip, c, p)
            if cores > 1:
                across(src, span, chip, p).wait_send()
                wait_block(span, chip, (c + 1) % cores, p)
            pl.when(has_up & (chip <= z))(lambda: up(src, span, chip, p).wait_send())
            pl.when(has_down & (chip >= z))(lambda: down(src, span, chip, p).wait_send())
        return 0

    lax.fori_loop(0, spans * chips, finish, 0)


def gather(rows, rotary_t):
    spans, heads = lax.axis_size("span"), lax.axis_size("heads")
    cores = 2 if heads % 2 == 0 else 1
    chips = heads // cores
    block, width = rows.shape[1:]
    pieces = PIECES if block % (16 * PIECES) == 0 else 1
    parts = pieces + 1
    dma = pltpu.SemaphoreType.DMA
    return pl.pallas_call(
        functools.partial(gather_kernel, (spans, chips, cores, pieces)),
        out_shape=(
            OUT((spans, heads, block, width), rows.dtype),
            OUT((spans, heads) + rotary_t.shape[1:], rotary_t.dtype),
        ),
        in_specs=[pl.BlockSpec(memory_space=pl.ANY)] * 2,
        out_specs=[pl.BlockSpec(memory_space=OUT_SPACE)] * 2,
        scratch_shapes=[
            dma((spans, heads, parts)),
            dma((spans, parts)),
            dma((spans, chips, parts)),
            dma((spans, chips, parts)),
            dma((spans, chips, parts)),
            dma((parts,)),
        ],
        compiler_params=pltpu.CompilerParams(
            collective_id=0, has_side_effects=True, vmem_limit_bytes=4 << 20
        ),
        name="gather",
    )(rows, rotary_t)


OUT = pltpu.VMEM
OUT_SPACE = pltpu.VMEM


def expand_kernel(group, rows_ref, rotary_ref, gain_ref, key_ref, value_ref, keys_out, values_out, mix):
    tile = pl.program_id(0)
    rows = rows_ref[pl.ds(tile * group, group)]
    rows = rows.reshape(-1, rows.shape[-1]).astype(jnp.float32)
    scale = lax.rsqrt(jnp.mean(rows * rows, axis=-1, keepdims=True) + 1e-06)
    ready = (rows * scale * gain_ref[...]).astype(jnp.bfloat16)
    count = ready.shape[0]
    heads, key_part = keys_out.shape[0], key_ref.shape[0] // keys_out.shape[0]
    keys = lax.dot_general(
        key_ref[...], ready, (((1,), (1,)), ((), ())), preferred_element_type=jnp.float32
    ).astype(jnp.bfloat16)
    values = jnp.dot(ready, value_ref[...], preferred_element_type=jnp.float32)
    turned = jnp.concatenate([rotary_ref[tile * group + g] for g in range(group)], axis=-1)
    size = values.shape[-1] // heads
    for h in range(heads):
        keys_out[h, :key_part] = keys[h * key_part : (h + 1) * key_part]
        keys_out[h, key_part:] = turned
        mix[pl.ds(h, count, stride=heads)] = values[:, h * size : (h + 1) * size]
    values_out[...] = mix[...].astype(values_out.dtype)


def expand(rows, rotary_t, gain, key_up, value_up):
    blocks, block, width = rows.shape
    heads, key_part = key_up.shape[1:]
    size = value_up.shape[2]
    turn = rotary_t.shape[1]
    group = 1
    while blocks % (2 * group) == 0 and (block * group < 768 or block * group % 128):
        group *= 2
    count = block * group
    whole = pl.BlockSpec(memory_space=pltpu.VMEM)
    keys, values = pl.pallas_call(
        functools.partial(expand_kernel, group),
        grid=(blocks // group,),
        out_shape=(
            jax.ShapeDtypeStruct((heads, key_part + turn, blocks * block), rows.dtype),
            jax.ShapeDtypeStruct((blocks * block * heads, size), rows.dtype),
        ),
        in_specs=[whole] * 5,
        out_specs=(
            pl.BlockSpec((heads, key_part + turn, count), lambda t: (0, 0, t)),
            pl.BlockSpec((count * heads, size), lambda t: (t, 0)),
        ),
        scratch_shapes=[pltpu.VMEM((count * heads, size), jnp.float32)],
        compiler_params=pltpu.CompilerParams(vmem_limit_bytes=24 << 20),
        name="expand",
    )(
        rows,
        rotary_t,
        gain[None],
        key_up.reshape(width, heads * key_part).T,
        value_up.reshape(width, heads * size),
    )
    stored_keys = keys.transpose(2, 0, 1)[None]
    return stored_keys, values.reshape(1, blocks * block, heads, size)


def per_device(latents, rotary_rows, latent_gain, key_up, value_up):
    rows, rotary = gather(latents, rotary_rows.transpose(0, 2, 1))
    rows = rows.reshape((-1,) + rows.shape[2:])
    rotary = rotary.reshape((-1,) + rotary.shape[2:])
    return expand(rows, rotary, latent_gain, key_up, value_up)


def solution(mesh):
    in_specs = (
        P(None, ("span", "heads"), None),
        P(None, ("span", "heads"), None),
        P(),
        P(None, "heads", None),
        P(None, "heads", None),
    )
    out_specs = (P("span", None, "heads", None), P("span", None, "heads", None))
    return jax.shard_map(
        per_device, mesh=mesh, in_specs=in_specs, out_specs=out_specs, check_vma=False
    )
```

time: 149 us -> 82.8 us (0.56)
  Pallas kernels: 0 us -> 77.1 us
  blocking collectives: 47.8 us -> 0 us
  waiting for transfers between devices: 40.2 us -> 0 us
  local copies, waits for them, and re-layouts: 30.9 us -> 4.81 us
  between operations: 14.2 us -> 0.67 us
  matrix products: 6.41 us -> 0 us
  other arithmetic: 5.74 us -> 0 us
  starting transfers between devices: 3.38 us -> 0 us
    pallas_call x0 -> x2, Pallas kernels: none -> 77.1 us  [the longest x1 69.6 us: gather(): pl.pallas_call(functools.partial(gather_kernel, (spans, chips, cores, pie...]
    all_gather x1 -> x0, waiting for transfers between devices: 35.4 us -> none  [per_device(): lax.all_gather(rows_cut, 'heads', axis=2, tiled=True)]
    all_gather x1 -> x0, blocking collectives: 31.4 us -> none  [per_device(): lax.all_gather(rotary_cut, 'heads', axis=2, tiled=True)]
    unnamed x9 -> x8, local copies, waits for them, and re-layouts: 29.4 us -> 4.81 us
    all_to_all x1 -> x0, blocking collectives: 16.5 us -> none  [per_device(): lax.all_to_all(rows_ready, 'span', split_axis=0, concat_axis=1, tiled=True)]
    all_to_all x1 -> x0, waiting for transfers between devices: 4.81 us -> none  [per_device(): lax.all_to_all(rotary_rows, 'span', split_axis=0, concat_axis=1, tiled=True)]
    unnamed x1 -> x0, matrix products: 4.61 us -> none
    all_to_all x1 -> x0, starting transfers between devices: 3.34 us -> none  [per_device(): lax.all_to_all(rotary_rows, 'span', split_axis=0, concat_axis=1, tiled=True)]
  transfers between devices with their start and end apart: 2 -> 0, of which waited for: 2 -> 0; matrix products, arithmetic and copies ran while one was open for 1% -> 0% of each run, Pallas kernels for 0% -> 0%
where the time goes in v1:
time: 82.8 us; the launch traced here: 82.6 us
  Pallas kernels  77.1 us (93%)
  local copies, waits for them, and re-layouts  4.81 us (6%)
    pallas_call x1, Pallas kernels, gather(): pl.pallas_call(functools.partial(gather_kernel, (spans, chips, cores, pie...  69.6 us
    pallas_call x1, Pallas kernels, expand(): pl.pallas_call(functools.partial(expand_kernel, group), grid=(blocks // g...  7.51 us
    unnamed x8, local copies, waits for them, and re-layouts  4.81 us

profile of v1, /device:TPU:0, one launch (start us, length us, event | category | flops | bytes accessed | tf_op | source)
XLA Modules:
  0.0 82.6 jit_solution(8976149486015311072)
XLA Ops:
  0.6 1.1 %copy.7 = bf16[512,2,128]{0,2,1:T(8,128)(2,1)S(1)} copy(bf16[512,2,128]{2,1,0:T(2,128)(2,1)} %param.8) | data formatting | bytes 524288 | tf_op args[3]
  1.7 1.0 %copy.10 = bf16[64,8,2,128]{3,1,2,0:T(8,128)(2,1)S(1)} copy(bf16[64,8,2,128]{3,2,1,0:T(2,128)(2,1)} %bitcast.21) | data formatting | bytes 524288
  2.7 0.0 copy-start
  2.8 1.1 %copy-done = bf16[4,192,512]{2,1,0:T(8,128)(2,1)S(1)} copy-done((bf16[4,192,512]{2,1,0:T(8,128)(2,1)S(1)}, bf16[4,192,512]{2,1,0:T(8,128)(2,1)}, u32[]{:S(2)}) %copy-start) | copy-done | bytes 786456
  3.9 0.0 copy-start.1
  3.9 0.9 %copy-done.1 = bf16[4,192,64]{1,2,0:T(8,128)(2,1)S(1)} copy-done((bf16[4,192,64]{1,2,0:T(8,128)(2,1)S(1)}, bf16[4,192,64]{1,2,0:T(8,128)(2,1)}, u32[]{:S(2)}) %copy-start.1) | copy-done | bytes 98328
  4.8 69.6 %gather.1 = (bf16[4,8,192,512]{3,2,1,0:T(8,128)(2,1)S(1)}, bf16[4,8,64,192]{3,2,1,0:T(8,128)(2,1)S(1)}) custom-call(bf16[4,192,512]{2,1,0:T(8,128)(2,1)S(1)} %copy-done, bf16[4,64,192]{2,1,0:T(8,128)(2,1)S(1)} %bitcast.19), custom_call_target="tpu_custom_call" | custom-call | tf_op jit(solution)/shard_map/gather/pallas_call | solution.py:177
  74.4 0.0 copy-start.2
  74.4 0.7 copy-done.2
  75.0 7.5 %expand.1 = (bf16[2,192,6144]{2,1,0:T(8,128)(2,1)}, bf16[12288,128]{1,0:T(8,128)(2,1)}) custom-call(bf16[32,192,512]{2,1,0:T(8,128)(2,1)S(1)} %bitcast.15, bf16[32,64,192]{2,1,0:T(8,128)(2,1)S(1)} %bitcast.16, f32[1,512]{1,0:T(1,128)S(1)} %bitcast.20, bf16[256,512]{1,0:T(8,128)(2,1)S(1)} %bitcast.17, bf16[512,256]{1,0:T(8,128)(2,1)S(1)} %bitcast.18), custom_call_target="tpu_custom_call" | custom-call | tf_op jit(solution)/shard_map/expand/pallas_call | solution.py:235
Async XLA Ops:
  2.7 1.1 %copy-start = (bf16[4,192,512]{2,1,0:T(8,128)(2,1)S(1)}, bf16[4,192,512]{2,1,0:T(8,128)(2,1)}, u32[]{:S(2)}) copy-start(bf16[4,192,512]{2,1,0:T(8,128)(2,1)} %rows_ref.1) | copy-start | bytes 2359300
  3.9 0.9 %copy-start.1 = (bf16[4,192,64]{1,2,0:T(8,128)(2,1)S(1)}, bf16[4,192,64]{1,2,0:T(8,128)(2,1)}, u32[]{:S(2)}) copy-start(bf16[4,192,64]{1,2,0:T(8,128)(2,1)} %param.6) | copy-start | bytes 294916
  74.4 0.7 copy-start.2

commit v2 on v1

--- a/solution.py
+++ b/solution.py
@@ -258,7 +258,294 @@
     return stored_keys, values.reshape(1, blocks * block, heads, size)
 
 
+def fused_kernel(
+    sizes, rows_ref, rotary_ref, gain_ref, key_ref, value_ref, keys_out, values_out, *scratch
+):
+    spans, chips, cores, pieces, packed = sizes
+    held, turned_held, rows_in, gain, key_in, value_in, wide, key_t, value_w, mix = scratch[:10]
+    recv_sem, plane_sem, up_sem, down_sem, partner_sem, own_sem, load_sem = scratch[10:]
+    block, width = rows_ref.shape[1:]
+    cut = block // pieces
+    me_s = lax.axis_index("span")
+    me_h = lax.axis_index("heads")
+    z, c = me_h // cores, me_h % cores
+    other = (c + 1) % cores
+    parts = range(pieces + 1)
+
+    def span_of(i):
+        if spans & (spans - 1):
+            return (me_s + i) % spans
+        total, bit = 0, 1
+        while bit < spans:
+            total = total + ((me_s // bit + i // bit) % 2) * bit
+            bit *= 2
+        return total
+
+    def to(span, heads):
+        return {"span": span, "heads": heads}
+
+    def slot(span, chip, core, piece):
+        if piece < pieces:
+            return held.at[span, chip * cores + core, pl.ds(piece * cut, cut)]
+        return turned_held.at[span, chip * cores + core]
+
+    def mine(i, piece):
+        if piece < pieces:
+            return rows_in.at[span_of(i), pl.ds(piece * cut, cut)]
+        return rotary_ref.at[span_of(i)]
+
+    def arrived(span, chip, core, piece):
+        return recv_sem.at[span, chip * cores + core, piece]
+
+    def push(src, span, chip, piece, send_sem, device):
+        return pltpu.make_async_remote_copy(
+            src_ref=src,
+            dst_ref=slot(span, chip, c, piece),
+            send_sem=send_sem,
+            recv_sem=arrived(span, chip, c, piece),
+            device_id=device,
+            device_id_type=MESH,
+        )
+
+    def wait_block(span, chip, core, piece):
+        ref = slot(span, chip, core, piece)
+        pltpu.make_async_remote_copy(
+            src_ref=ref,
+            dst_ref=ref,
+            send_sem=arrived(span, chip, core, piece),
+            recv_sem=arrived(span, chip, core, piece),
+            device_id=to(me_s, me_h),
+            device_id_type=MESH,
+        ).wait_recv()
+
+    def up(src, span, chip, p):
+        return push(src, span, chip, p, up_sem.at[span, chip, p], to(me_s, me_h + cores))
+
+    def down(src, span, chip, p):
+        return push(src, span, chip, p, down_sem.at[span, chip, p], to(me_s, me_h - cores))
+
+    def across(src, span, chip, p):
+        device = to(me_s, z * cores + other)
+        return push(src, span, chip, p, partner_sem.at[span, chip, p], device)
+
+    def plane(i, p):
+        device = to(span_of(i), me_h)
+        return push(mine(i, p), me_s, z, p, plane_sem.at[i, p], device)
+
+    has_up, has_down = z < chips - 1, z > 0
+
+    loads = [
+        pltpu.make_async_copy(rows_ref, rows_in, load_sem.at[0]),
+        pltpu.make_async_copy(rows_ref.at[me_s], held.at[me_s, me_h], load_sem.at[1]),
+        pltpu.make_async_copy(rotary_ref.at[me_s], turned_held.at[me_s, me_h], load_sem.at[2]),
+        pltpu.make_async_copy(gain_ref, gain, load_sem.at[3]),
+        pltpu.make_async_copy(key_ref, key_in, load_sem.at[4]),
+        pltpu.make_async_copy(value_ref, value_in, load_sem.at[5]),
+    ]
+    for load in loads:
+        load.start()
+
+    barrier = pltpu.get_barrier_semaphore()
+
+    def greet(device):
+        pl.semaphore_signal(barrier, inc=1, device_id=device, device_id_type=MESH)
+
+    for i in range(1, spans):
+        greet(to(span_of(i), me_h))
+    if cores > 1:
+        greet(to(me_s, z * cores + other))
+    pl.when(has_up)(lambda: greet(to(me_s, me_h + cores)))
+    pl.when(has_down)(lambda: greet(to(me_s, me_h - cores)))
+    loads[0].wait()
+    peers = spans - 1 + (cores > 1) + jnp.where(has_up, 1, 0) + jnp.where(has_down, 1, 0)
+    pl.semaphore_wait(barrier, peers)
+
+    def spread(src, span, chip, p, upward, downward):
+        pl.when(upward)(lambda: up(src, span, chip, p).start())
+        pl.when(downward)(lambda: down(src, span, chip, p).start())
+        if cores > 1:
+            across(src, span, chip, p).start()
+
+    for p in parts:
+        spread(mine(0, p), me_s, z, p, has_up, has_down)
+        for i in range(1, min(spans, 3)):
+            plane(i, p).start()
+    for i in range(3, spans):
+        for p in parts:
+            plane(i, p).start()
+
+    for load in loads[1:]:
+        load.wait()
+    heads, turn = keys_out.shape[0], turned_rows(turned_held.shape[2:], block)
+    key_part = keys_out.shape[1] - turn
+    size = values_out.shape[1]
+    wide[...] = key_in[...].astype(jnp.float32)
+    for h in range(heads):
+        key_t[h * key_part : (h + 1) * key_part] = (
+            wide[pl.ds(h, width, stride=heads)].T.astype(key_t.dtype)
+        )
+    wide[...] = value_in[...].astype(jnp.float32)
+    for h in range(heads):
+        value_w[:, h * size : (h + 1) * size] = (
+            wide[pl.ds(h, width, stride=heads)].astype(value_w.dtype)
+        )
+
+    def turned(span, head):
+        rows = turned_held[span, head]
+        if not packed:
+            return rows
+        tail = rows[turn:]
+        last = jnp.concatenate([tail[:, : block % 128], tail[:, block % 128 :]], axis=0)
+        return jnp.concatenate([rows[:turn], last], axis=-1)
+
+    count = block * cores
+
+    def compute(span, chip):
+        if cores > 1:
+            for p in parts:
+                wait_block(span, chip, other, p)
+        first = chip * cores
+        rows = held[span, pl.ds(first, cores)].reshape(count, width).astype(jnp.float32)
+        scale = lax.rsqrt(jnp.mean(rows * rows, axis=-1, keepdims=True) + 1e-06)
+        ready = (rows * scale * gain[...]).astype(jnp.bfloat16)
+        keys = lax.dot_general(
+            key_t[...], ready, (((1,), (1,)), ((), ())), preferred_element_type=jnp.float32
+        ).astype(keys_out.dtype)
+        values = jnp.dot(ready, value_w[...], preferred_element_type=jnp.float32)
+        shared = jnp.concatenate([turned(span, first + k) for k in range(cores)], axis=-1)
+        unit = span * chips + chip
+        places = pl.ds(pl.multiple_of(unit * count, 128), count)
+        for h in range(heads):
+            keys_out[h, :key_part, places] = keys[h * key_part : (h + 1) * key_part]
+            keys_out[h, key_part:, places] = shared
+            mix[pl.ds(h, count, stride=heads)] = values[:, h * size : (h + 1) * size]
+        lines = pl.ds(pl.multiple_of(unit * count * heads, 128), count * heads)
+        values_out[lines] = mix[...].astype(values_out.dtype)
+
+    def first_step(i, _):
+        span = span_of(i)
+        for p in parts:
+            wait_block(span, z, c, p)
+            spread(slot(span, z, c, p), span, z, p, has_up, has_down)
+        compute(span_of(i - 1), z)
+        return 0
+
+    lax.fori_loop(1, spans, first_step, 0)
+
+    def later_step(step, _):
+        def forward():
+            r, span = step // spans, span_of(step % spans)
+
+            def pass_on(chip, upward, downward):
+                for p in parts:
+                    wait_block(span, chip, c, p)
+                    spread(slot(span, chip, c, p), span, chip, p, upward, downward)
+
+            pl.when(z - r >= 0)(lambda: pass_on(z - r, has_up, False))
+            pl.when(z + r < chips)(lambda: pass_on(z + r, False, has_down))
+
+        pl.when(step < spans * chips)(forward)
+        before = step - 1
+        r, span = before // spans, span_of(before % spans)
+        pl.when(z - r >= 0)(lambda: compute(span, z - r))
+        pl.when((r > 0) & (z + r < chips))(lambda: compute(span, z + r))
+        return 0
+
+    lax.fori_loop(spans, spans * chips + 1, later_step, 0)
+
+    for p in parts:
+        for i in range(1, spans):
+            plane(i, p).wait_send()
+
+    def finish(step, _):
+        span, chip = step % spans, step // spans
+        for p in parts:
+            src = slot(span, chip, c, p)
+            if cores > 1:
+                across(src, span, chip, p).wait_send()
+            pl.when(has_up & (chip <= z))(lambda: up(src, span, chip, p).wait_send())
+            pl.when(has_down & (chip >= z))(lambda: down(src, span, chip, p).wait_send())
+        return 0
+
+    lax.fori_loop(0, spans * chips, finish, 0)
+
+
+def turned_rows(shape, block):
+    return shape[0] * shape[1] // block
+
+
+def fused(rows, rotary, gain, key_up, value_up, cores):
+    spans, heads = lax.axis_size("span"), lax.axis_size("heads")
+    chips = heads // cores
+    batch, block, width = rows.shape
+    mine, key_part = key_up.shape[1:]
+    size = value_up.shape[2]
+    turn = rotary.shape[2]
+    rotary = rotary.transpose(0, 2, 1)
+    packed = block == 192 and turn % 32 == 0
+    if packed:
+        full = block - block % 128
+        tail = jnp.concatenate(
+            [rotary[:, : turn // 2, full:], rotary[:, turn // 2 :, full:]], axis=2
+        )
+        rotary = jnp.concatenate(
+            [rotary[:, :, k : k + 128] for k in range(0, full, 128)] + [tail], axis=1
+        )
+    pieces = PIECES if block % (16 * PIECES) == 0 else 1
+    parts = pieces + 1
+    total = spans * heads * block
+    dma = pltpu.SemaphoreType.DMA
+    hbm = pl.BlockSpec(memory_space=pltpu.HBM)
+    vmem = pl.BlockSpec(memory_space=pltpu.VMEM)
+    bf16, f32 = rows.dtype, jnp.float32
+    beside = 2 * total * mine * (key_part + turn + size) + 2 * rotary.size
+    grant = (67043328 - beside - (64 << 10)) // 4096 * 4096
+    keys, values = pl.pallas_call(
+        functools.partial(fused_kernel, (spans, chips, cores, pieces, packed)),
+        out_shape=(
+            pltpu.VMEM((mine, key_part + turn, total), bf16),
+            pltpu.VMEM((total * mine, size), bf16),
+        ),
+        in_specs=[hbm, vmem, hbm, hbm, hbm],
+        out_specs=[vmem] * 2,
+        scratch_shapes=[
+            pltpu.VMEM((spans, heads, block, width), bf16),
+            pltpu.VMEM((spans, heads) + rotary.shape[1:], bf16),
+            pltpu.VMEM(rows.shape, bf16),
+            pltpu.VMEM((1, width), f32),
+            pltpu.VMEM((width * mine, key_part), bf16),
+            pltpu.VMEM((width * mine, size), bf16),
+            pltpu.VMEM((width * mine, max(key_part, size)), f32),
+            pltpu.VMEM((mine * key_part, width), bf16),
+            pltpu.VMEM((width, mine * size), bf16),
+            pltpu.VMEM((block * cores * mine, size), f32),
+            dma((spans, heads, parts)),
+            dma((spans, parts)),
+            dma((spans, chips, parts)),
+            dma((spans, chips, parts)),
+            dma((spans, chips, parts)),
+            dma((parts,)),
+            dma((6,)),
+        ],
+        compiler_params=pltpu.CompilerParams(
+            collective_id=0, has_side_effects=True, vmem_limit_bytes=grant
+        ),
+        name="fused",
+    )(
+        rows,
+        rotary,
+        gain[None],
+        key_up.reshape(width * mine, key_part),
+        value_up.reshape(width * mine, size),
+    )
+    stored_keys = keys.transpose(2, 0, 1)[None]
+    return stored_keys, values.reshape(1, total, mine, size)
+
+
 def per_device(latents, rotary_rows, latent_gain, key_up, value_up):
+    cores = 2 if lax.axis_size("heads") % 2 == 0 else 1
+    if latents.shape[1] * cores % 128 == 0 and key_up.shape[2] == value_up.shape[2]:
+        return fused(latents, rotary_rows, latent_gain, key_up, value_up, cores)
     rows, rotary = gather(latents, rotary_rows.transpose(0, 2, 1))
     rows = rows.reshape((-1,) + rows.shape[2:])
     rotary = rotary.reshape((-1,) + rotary.shape[2:])

time: 82.8 us -> 74.8 us (0.903)
  Pallas kernels: 77.1 us -> 67.7 us
    pallas_call x2 -> x1, Pallas kernels: 77.1 us -> 67.7 us  [fused(): pl.pallas_call(functools.partial(fused_kernel, (spans, chips, cores, piec...]
    slice x0 -> x2, local copies, waits for them, and re-layouts: none -> 1.63 us  [the longest x1 0.85 us: fused(): rotary[:, :, k:k + 128]]
    unnamed x8 -> x2, local copies, waits for them, and re-layouts: 4.81 us -> 3.85 us
where the time goes in v2:
time: 74.8 us; the launch traced here: 74.5 us
  Pallas kernels  67.7 us (91%)
  local copies, waits for them, and re-layouts  5.48 us (7%)
    pallas_call x1, Pallas kernels, fused(): pl.pallas_call(functools.partial(fused_kernel, (spans, chips, cores, piec...  67.7 us
    unnamed x2, local copies, waits for them, and re-layouts  3.85 us

profile of v2, /device:TPU:0, one launch (start us, length us, event | category | flops | bytes accessed | tf_op | source)
XLA Modules:
  0.0 74.5 jit_solution(11113617303321586947)
XLA Ops:
  0.6 0.8 %slice.12 = bf16[4,64,128]{2,1,0:T(8,128)(2,1)S(1)} slice(bf16[4,64,192]{2,1,0:T(8,128)(2,1)} %bitcast.12), slice={[0:4], [0:64], [0:128]} | slice | bytes 131072 | tf_op jit(solution)/shard_map/slice | solution.py:492
  1.5 0.8 %fusion = (bf16[4,32,64]{2,1,0:T(8,128)(2,1)S(1)}, bf16[4,32,64]{2,1,0:T(8,128)(2,1)S(1)}) fusion(bf16[4,64,192]{2,1,0:T(8,128)(2,1)} %bitcast.13), kind=kLoop, calls=%fused_computation.1 | loop fusion | bytes 65536 | tf_op jit(solution)/shard_map/slice | solution.py:489
  2.3 0.7 maximum_maximum_fusion.rotary_ref
  3.0 67.7 %fused.1 = (bf16[2,192,6144]{2,1,0:T(8,128)(2,1)S(1)}, bf16[12288,128]{1,0:T(8,128)(2,1)S(1)}) custom-call(bf16[4,192,512]{2,1,0:T(8,128)(2,1)} %rows_ref.1, bf16[4,96,128]{2,1,0:T(8,128)(2,1)} %maximum_maximum_fusion.rotary_ref, f32[1,512]{1,0:T(1,128)} %bitcast.14, bf16[1024,128]{1,0:T(8,128)(2,1)} %bitcast.10, bf16[1024,128]{1,0:T(8,128)(2,1)} %bitcast.11), custom_call_target="tpu_custom_call" | custom-call | tf_op jit(solution)/shard_map/fused/pallas_call | solution.py:503
  70.7 2.2 %copy.9 = bf16[1,6144,2,192]{1,3,2,0:T(8,128)(2,1)} copy(bf16[1,6144,2,192]{1,3,2,0:T(8,128)(2,1)S(1)} %bitcast.8) | data formatting | bytes 9437184
  72.8 1.7 %copy.10 = bf16[1,6144,2,128]{3,2,1,0:T(2,128)(2,1)} copy(bf16[1,6144,2,128]{3,2,1,0:T(2,128)(2,1)S(1)} %bitcast.9) | data formatting | bytes 6291456

commit v3 on v2

--- a/solution.py
+++ b/solution.py
@@ -9,6 +9,7 @@
 
 MESH = pl.DeviceIdType.MESH
 PIECES = 2
+OUT_PIECES = 4
 
 
 def gather_kernel(sizes, rows_ref, rotary_ref, rows_out, rotary_out, *sems):
@@ -444,11 +445,11 @@
             pl.when(z - r >= 0)(lambda: pass_on(z - r, has_up, False))
             pl.when(z + r < chips)(lambda: pass_on(z + r, False, has_down))
 
-        pl.when(step < spans * chips)(forward)
         before = step - 1
         r, span = before // spans, span_of(before % spans)
         pl.when(z - r >= 0)(lambda: compute(span, z - r))
         pl.when((r > 0) & (z + r < chips))(lambda: compute(span, z + r))
+        pl.when(step < spans * chips)(forward)
         return 0
 
     lax.fori_loop(spans, spans * chips + 1, later_step, 0)
@@ -468,6 +469,60 @@
         return 0
 
     lax.fori_loop(0, spans * chips, finish, 0)
+
+
+def pack_kernel(turn, rows_ref, packed_ref):
+    half, full = turn // 2, packed_ref.shape[2]
+    rest = full // 2
+    for b in range(rows_ref.shape[0]):
+        packed_ref[b, :turn] = rows_ref[b, :, :full]
+        packed_ref[b, turn:, :rest] = rows_ref[b, :half, full:]
+        packed_ref[b, turn:, rest:] = rows_ref[b, half:, full:]
+
+
+def pack(rotary, block):
+    batch, turn = rotary.shape[:2]
+    vmem = pl.BlockSpec(memory_space=pltpu.VMEM)
+    return pl.pallas_call(
+        functools.partial(pack_kernel, turn),
+        out_shape=pltpu.VMEM((batch, turn * block // 128, 128), rotary.dtype),
+        in_specs=[vmem],
+        out_specs=vmem,
+        compiler_params=pltpu.CompilerParams(vmem_limit_bytes=4 << 20),
+        name="pack",
+    )(rotary)
+
+
+def copy_out_kernel(pieces, keys_ref, values_ref, keys_out, values_out, sem):
+    copies = []
+    for src, dst in ((keys_ref, keys_out), (values_ref, values_out)):
+        step = src.shape[-2] // pieces
+        for k in range(pieces):
+            for h in range(src.shape[0] if len(src.shape) == 3 else 1):
+                rows = pl.ds(k * step, step)
+                at = (h, rows) if len(src.shape) == 3 else (rows,)
+                copies.append(
+                    pltpu.make_async_copy(src.at[at], dst.at[at], sem.at[len(copies)])
+                )
+    for copy in copies:
+        copy.start()
+    for copy in copies:
+        copy.wait()
+
+
+def copy_out(keys, values):
+    pieces = OUT_PIECES
+    vmem = pl.BlockSpec(memory_space=pltpu.VMEM)
+    hbm = pl.BlockSpec(memory_space=pltpu.HBM)
+    return pl.pallas_call(
+        functools.partial(copy_out_kernel, pieces),
+        out_shape=[jax.ShapeDtypeStruct(x.shape, x.dtype) for x in (keys, values)],
+        in_specs=[vmem] * 2,
+        out_specs=[hbm] * 2,
+        scratch_shapes=[pltpu.SemaphoreType.DMA((pieces * (keys.shape[0] + 1),))],
+        compiler_params=pltpu.CompilerParams(vmem_limit_bytes=1 << 20),
+        name="copy_out",
+    )(keys, values)
 
 
 def turned_rows(shape, block):
@@ -484,13 +539,7 @@
     rotary = rotary.transpose(0, 2, 1)
     packed = block == 192 and turn % 32 == 0
     if packed:
-        full = block - block % 128
-        tail = jnp.concatenate(
-            [rotary[:, : turn // 2, full:], rotary[:, turn // 2 :, full:]], axis=2
-        )
-        rotary = jnp.concatenate(
-            [rotary[:, :, k : k + 128] for k in range(0, full, 128)] + [tail], axis=1
-        )
+        rotary = pltpu.with_memory_space_constraint(pack(rotary, block), pltpu.VMEM)
     pieces = PIECES if block % (16 * PIECES) == 0 else 1
     parts = pieces + 1
     total = spans * heads * block
@@ -499,7 +548,7 @@
     vmem = pl.BlockSpec(memory_space=pltpu.VMEM)
     bf16, f32 = rows.dtype, jnp.float32
     beside = 2 * total * mine * (key_part + turn + size) + 2 * rotary.size
-    grant = (67043328 - beside - (64 << 10)) // 4096 * 4096
+    grant = (67043328 - beside - (224 << 10)) // 4096 * 4096
     keys, values = pl.pallas_call(
         functools.partial(fused_kernel, (spans, chips, cores, pieces, packed)),
         out_shape=(
@@ -538,6 +587,7 @@
         key_up.reshape(width * mine, key_part),
         value_up.reshape(width * mine, size),
     )
+    keys, values = copy_out(keys, values)
     stored_keys = keys.transpose(2, 0, 1)[None]
     return stored_keys, values.reshape(1, total, mine, size)
 

time: 74.8 us -> 71.9 us (0.961)
  local copies, waits for them, and re-layouts: 5.48 us -> 0.9 us
  Pallas kernels: 67.7 us -> 69.5 us
    pallas_call x0 -> x2, Pallas kernels: none -> 3.33 us  [the longest x1 3.25 us: copy_out(): pl.pallas_call(functools.partial(copy_out_kernel, pieces), out_shape=[jax...]
    unnamed x2, local copies, waits for them, and re-layouts: 3.85 us -> 0.9 us
    slice x2 -> x0, local copies, waits for them, and re-layouts: 1.63 us -> none  [the longest x1 0.85 us: fused(): rotary[:, :, k:k + 128]]
    pallas_call x1, Pallas kernels: 67.7 us -> 66.2 us  [fused(): pl.pallas_call(functools.partial(fused_kernel, (spans, chips, cores, piec...]
where the time goes in v3:
time: 71.9 us; the launch traced here: 71.1 us
  Pallas kernels  69.5 us (97%)
  local copies, waits for them, and re-layouts  0.9 us (1%)
    pallas_call x1, Pallas kernels, fused(): pl.pallas_call(functools.partial(fused_kernel, (spans, chips, cores, piec...  66.2 us
    pallas_call x1, Pallas kernels, copy_out(): pl.pallas_call(functools.partial(copy_out_kernel, pieces), out_shape=[jax...  3.25 us

profile of v3, /device:TPU:0, one launch (start us, length us, event | category | flops | bytes accessed | tf_op | source)
XLA Modules:
  0.0 71.1 jit_solution(17204714981719886840)
XLA Ops:
  0.6 0.0 copy-start
  0.6 0.9 %copy-done = bf16[4,192,64]{1,2,0:T(8,128)(2,1)S(1)} copy-done((bf16[4,192,64]{1,2,0:T(8,128)(2,1)S(1)}, bf16[4,192,64]{1,2,0:T(8,128)(2,1)}, u32[]{:S(2)}) %copy-start) | copy-done | bytes 98328
  1.5 0.1 pack.1.rotary_ref
  1.6 66.2 %fused.1 = (bf16[2,192,6144]{2,1,0:T(8,128)(2,1)S(1)}, bf16[12288,128]{1,0:T(8,128)(2,1)S(1)}) custom-call(bf16[4,192,512]{2,1,0:T(8,128)(2,1)} %rows_ref.1, bf16[4,96,128]{2,1,0:T(8,128)(2,1)S(1)} %pack.1.rotary_ref, f32[1,512]{1,0:T(1,128)} %bitcast.11, bf16[1024,128]{1,0:T(8,128)(2,1)} %bitcast.9, bf16[1024,128]{1,0:T(8,128)(2,1)} %bitcast.10), custom_call_target="tpu_custom_call" | custom-call | tf_op jit(solution)/shard_map/fused/pallas_call | solution.py:552
  67.8 3.2 %copy_out.1 = (bf16[2,192,6144]{2,1,0:T(8,128)(2,1)}, bf16[12288,128]{1,0:T(8,128)(2,1)}) custom-call(bf16[2,192,6144]{2,1,0:T(8,128)(2,1)S(1)} %get-tuple-element.6.keys_ref, bf16[12288,128]{1,0:T(8,128)(2,1)S(1)} %get-tuple-element.7.values_ref), custom_call_target="tpu_custom_call" | custom-call | tf_op jit(solution)/shard_map/copy_out/pallas_call | solution.py:517
Async XLA Ops:
  0.6 0.9 %copy-start = (bf16[4,192,64]{1,2,0:T(8,128)(2,1)S(1)}, bf16[4,192,64]{1,2,0:T(8,128)(2,1)}, u32[]{:S(2)}) copy-start(bf16[4,192,64]{1,2,0:T(8,128)(2,1)} %param.6) | copy-start | bytes 294916
